TPU v7x, 32 devices: a whole 2x2x4 slice. The times are simulated.
32 devices in a mesh: dp: 4 (over y, core), seq: 8 (over z, x).
Axes of the slice: x: 2, y: 2, z: 4, core: 2. Of those that a mesh axis runs over, the one named last changes fastest.
Arguments:
- queries: bfloat16 [32, 2048, 512], P('dp', 'seq'), may hold values from -6 to 6
- enc_keys: bfloat16 [32, 2048, 512], P('dp', 'seq'), may hold values from -6 to 6
- enc_values: bfloat16 [32, 2048, 512], P('dp', 'seq'), may hold values from -6 to 6
- dec_ids: int32 [32, 2048], P('dp', 'seq'), may hold values from 0 to 15, never falling along the last dimension, each value on 1 to 512 neighbouring positions
- enc_ids: int32 [32, 2048], P('dp', 'seq'), may hold values from 0 to 15, never falling along the last dimension, each value on 1 to 512 neighbouring positions
Outputs:
- context: bfloat16 [32, 2048, 512], P('dp', 'seq')
Inputs may be any that keep to these rules, and one draw needn't show every extreme that they name: `dec_ids`: along each row the numbers never fall; every number from 0 to 15 occurs in every row; a document holds 1 to 512 positions of a row, and some document holds exactly 512. `enc_ids`: along each row the numbers never fall; every number from 0 to 15 occurs in every row; a document holds 1 to 512 positions of a row, and some document holds exactly 512.
All inputs are finite; a program needn't handle non-finite values.
Results may differ from a plain program's by a relative error of at most 0.0047.
Values may be sent and summed in bfloat16 or wider, within the bound.
No kernel may reach another device: no remote copies, remote signals or barrier semaphores. Data moves between devices by JAX's collectives and lax.ppermute only.
A program may use at most 128 MiB of HBM per device.

v0:
```python
import jax
import jax.numpy as jnp
from jax import lax
from jax.sharding import PartitionSpec as P

HEAD_DIM = 64
masked_score = -1e30


def shortened(value):

    def short(part):
        return part.astype(jnp.bfloat16) if part.dtype == jnp.float32 else part

    return jax.tree.map(short, value)


def attend_dense(query_row, key_row, value_row, dec_row, enc_row, head_count):
    length = query_row.shape[0]
    query_heads = query_row.reshape(length, head_count, HEAD_DIM)
    key_heads = key_row.reshape(length, head_count, HEAD_DIM)
    value_heads = value_row.reshape(length, head_count, HEAD_DIM)
    query_span = min(512, length)
    pieces = []
    for offset in range(0, length, query_span):
        scores = jnp.einsum(
            "qhd,khd->hqk",
            query_heads[offset : offset + query_span],
            key_heads,
            preferred_element_type=jnp.float32,
        )
        allowed = (dec_row[offset : offset + query_span][:, None] == enc_row[None, :])[None]
        scores = jnp.where(allowed, scores, masked_score)
        row_peak = jnp.max(scores, axis=2, keepdims=True)
        expos = jnp.where(allowed, jnp.exp(scores - row_peak), 0.0)
        row_total = jnp.sum(expos, axis=2, keepdims=True)
        weights = (expos / row_total).astype(jnp.bfloat16)
        summed = jnp.einsum(
            "hqk,khd->qhd", weights, value_heads, preferred_element_type=jnp.float32
        )
        pieces.append(summed.reshape(query_span, head_count * HEAD_DIM).astype(jnp.bfloat16))
    return jnp.concatenate(pieces, axis=0)


def local(queries, enc_keys, enc_values, dec_ids, enc_ids):
    group = lax.axis_size("seq")
    dec_spread = jnp.broadcast_to(
        dec_ids.astype(jnp.bfloat16)[:, :, None], (dec_ids.shape[0], dec_ids.shape[1], group)
    )
    enc_spread = jnp.broadcast_to(
        enc_ids.astype(jnp.bfloat16)[:, :, None], (enc_ids.shape[0], enc_ids.shape[1], group)
    )
    members = (
        lax.all_to_all(queries, "seq", split_axis=2, concat_axis=1, tiled=True),
        lax.all_to_all(enc_keys, "seq", split_axis=2, concat_axis=1, tiled=True),
        lax.all_to_all(enc_values, "seq", split_axis=2, concat_axis=1, tiled=True),
        lax.all_to_all(dec_spread, "seq", split_axis=2, concat_axis=1, tiled=True),
        lax.all_to_all(enc_spread, "seq", split_axis=2, concat_axis=1, tiled=True),
    )
    dec_rows = members[3][:, :, 0].astype(jnp.int32)
    enc_rows = members[4][:, :, 0].astype(jnp.int32)
    query_rows = members[0]
    key_rows = members[1]
    value_rows = members[2]
    head_count = query_rows.shape[2] // HEAD_DIM

    def one_row(members):
        return attend_dense(members[0], members[1], members[2], members[3], members[4], head_count)

    attended = lax.map(one_row, (query_rows, key_rows, value_rows, dec_rows, enc_rows))
    return lax.all_to_all(
        shortened(attended), "seq", split_axis=1, concat_axis=2, tiled=True
    ).astype(attended.dtype)


def solution(mesh):
    in_specs = (
        P("dp", "seq", None),
        P("dp", "seq", None),
        P("dp", "seq", None),
        P("dp", "seq"),
        P("dp", "seq"),
    )
    out_specs = P("dp", "seq", None)
    return jax.shard_map(local, mesh=mesh, in_specs=in_specs, out_specs=out_specs, check_vma=False)
```

profile of v0, /device:TPU:0, one launch (start us, length us, event | category | flops | bytes accessed | tf_op | source)
XLA Modules:
  0.0 412.9 jit_solution(16733577638339409978)
XLA Ops:
  1.3 7.3 %all-to-all-start.1 = ((bf16[8,256,8]{1,0,2:T(8,128)(2,1)}), bf16[8,256,8]{1,0,2:T(8,128)(2,1)S(1)}, u32[]{:S(2)}, u32[]{:S(2)}) async-start(bf16[8,256,8]{1,0,2:T(8,128)(2,1)} %broadcast_in_dim.23), calls=%async_computation.1 | async-start | bytes 65536 | tf_op jit(solution)/shard_map/all_to_all | solution.py:57
  9.3 6.0 %all-to-all-done.1 = bf16[8,256,8]{1,0,2:T(8,128)(2,1)S(1)} async-done(((bf16[8,256,8]{1,0,2:T(8,128)(2,1)}), bf16[8,256,8]{1,0,2:T(8,128)(2,1)S(1)}, u32[]{:S(2)}, u32[]{:S(2)}) %all-to-all-start.1) | async-done | bytes 32800 | tf_op jit(solution)/shard_map/all_to_all | solution.py:57
  19.2 4.5 %copy.25 = bf16[8,256,512]{1,0,2:T(8,128)(2,1)} copy(bf16[8,256,512]{2,1,0:T(8,128)(2,1)} %param.9) | data formatting | bytes 4194304 | tf_op args[2]
  29.7 4.5 %copy.28 = bf16[8,256,512]{1,0,2:T(8,128)(2,1)} copy(bf16[8,256,512]{2,1,0:T(8,128)(2,1)} %param.7) | data formatting | bytes 4194304 | tf_op args[0]
  34.2 42.1 %all-to-all-done = bf16[8,256,512]{1,0,2:T(8,128)(2,1)S(1)} async-done(((bf16[8,256,512]{1,0,2:T(8,128)(2,1)}), bf16[8,256,512]{1,0,2:T(8,128)(2,1)S(1)}, u32[]{:S(2)}, u32[]{:S(2)}) %all-to-all-start) | async-done | bytes 2097184 | tf_op jit(solution)/shard_map/all_to_all | solution.py:56
  76.3 4.4 %all-to-all-start.3 = ((bf16[8,256,512]{1,0,2:T(8,128)(2,1)}), bf16[8,256,512]{1,0,2:T(8,128)(2,1)}, u32[]{:S(2)}, u32[]{:S(2)}) async-start(bf16[8,256,512]{1,0,2:T(8,128)(2,1)} %copy.28), calls=%async_computation.3 | async-start | bytes 4194304 | tf_op jit(solution)/shard_map/all_to_all | solution.py:54
  80.7 4.5 %copy.31 = bf16[8,256,512]{1,0,2:T(8,128)(2,1)} copy(bf16[8,256,512]{2,1,0:T(8,128)(2,1)} %param.8) | data formatting | bytes 4194304 | tf_op args[1]
  85.2 43.1 %all-to-all-done.3 = bf16[8,256,512]{1,0,2:T(8,128)(2,1)} async-done(((bf16[8,256,512]{1,0,2:T(8,128)(2,1)}), bf16[8,256,512]{1,0,2:T(8,128)(2,1)}, u32[]{:S(2)}, u32[]{:S(2)}) %all-to-all-start.3) | async-done | bytes 2097184 | tf_op jit(solution)/shard_map/all_to_all | solution.py:54
  128.3 4.4 %all-to-all-start.4 = ((bf16[8,256,512]{1,0,2:T(8,128)(2,1)}), bf16[8,256,512]{1,0,2:T(8,128)(2,1)}, u32[]{:S(2)}, u32[]{:S(2)}) async-start(bf16[8,256,512]{1,0,2:T(8,128)(2,1)} %copy.31), calls=%async_computation.4 | async-start | bytes 4194304 | tf_op jit(solution)/shard_map/all_to_all | solution.py:55
  136.3 5.0 %copy.44 = bf16[8,8,256,64]{3,2,1,0:T(8,128)(2,1)} copy(bf16[8,8,256,64]{2,0,3,1:T(8,128)(2,1)} %bitcast.36) | data formatting | bytes 4194304 | tf_op jit(solution)/shard_map/while | solution.py:70
  141.3 39.2 %all-to-all-done.4 = bf16[8,256,512]{1,0,2:T(8,128)(2,1)} async-done(((bf16[8,256,512]{1,0,2:T(8,128)(2,1)}), bf16[8,256,512]{1,0,2:T(8,128)(2,1)}, u32[]{:S(2)}, u32[]{:S(2)}) %all-to-all-start.4) | async-done | bytes 2097184 | tf_op jit(solution)/shard_map/all_to_all | solution.py:55
  180.5 5.0 %copy.46 = bf16[8,8,256,64]{3,2,1,0:T(8,128)(2,1)} copy(bf16[8,8,256,64]{2,0,3,1:T(8,128)(2,1)} %bitcast.40) | data formatting | bytes 4194304 | tf_op jit(solution)/shard_map/while | solution.py:70
  185.5 150.7 %while.10 = (s32[]{:T(128)}, bf16[8,2048,64]{1,2,0:T(8,128)(2,1)S(1)}, bf16[8,2048,64]{2,1,0:T(8,128)(2,1)}, s32[8,2048]{1,0:T(8,128)S(1)}, s32[8,2048]{1,0:T(8,...) while((s32[]{:T(128)}, ...), condition=%wide.region_9.10_spmd, body=%wide.region_0.9_spmd.sunk | while | flops 1133637632 | bytes 72773864 | solution.py:70
  191.2 3.9 fusion.85
  210.1 3.9 fusion.85
  228.9 3.9 fusion.85
  247.7 3.9 fusion.85
  266.6 3.9 fusion.85
  323.1 3.9 fusion.85
  336.2 4.3 %copy.37 = bf16[8,2048,64]{2,0,1:T(8,128)(2,1)} copy(bf16[8,2048,64]{1,2,0:T(8,128)(2,1)S(1)} %get-tuple-element.42) | data formatting | bytes 4194304 | tf_op jit(solution)/shard_map/while | solution.py:70
  340.5 6.4 %reshape.166 = bf16[8,2,65536]{2,1,0:T(2,128)(2,1)S(1)} reshape(bf16[2048,8,64]{2,1,0:T(8,128)(2,1)} %bitcast.147) | data formatting | bytes 4194304
  346.8 51.8 %all_to_all.90 = bf16[8,2,65536]{2,1,0:T(2,128)(2,1)} all-to-all(bf16[8,2,65536]{2,1,0:T(2,128)(2,1)S(1)} %reshape.166), channel_id=1, replica_groups=mesh['dp'=4,'seq'=8] {'seq'}, dimensions={0} | all-to-all | bytes 4194304 | tf_op jit(solution)/shard_map/all_to_all | solution.py:71
  398.7 7.4 %reshape.167 = bf16[2048,8,64]{2,1,0:T(8,128)(2,1)} reshape(bf16[8,2,65536]{2,1,0:T(2,128)(2,1)} %all_to_all.90) | data formatting | bytes 4194304
  406.1 4.5 %copy.39 = bf16[8,256,8,64]{1,3,2,0:T(8,128)(2,1)S(1)} copy(bf16[8,256,8,64]{3,0,1,2:T(8,128)(2,1)} %bitcast.148) | data formatting | bytes 4194304 | tf_op jit(solution)/shard_map/all_to_all | solution.py:71
  (120 shorter events, 144.7 us)
Async XLA Ops:
  1.3 14.0 %all-to-all-start.1 = ((bf16[8,256,8]{1,0,2:T(8,128)(2,1)}), bf16[8,256,8]{1,0,2:T(8,128)(2,1)S(1)}, u32[]{:S(2)}, u32[]{:S(2)}) async-start(bf16[8,256,8]{1,0,2:T(8,128)(2,1)} %broadcast_in_dim.23), calls=%async_computation.1 | async-start | bytes 65536 | tf_op jit(solution)/shard_map/all_to_all | solution.py:57
  15.9 10.0 %all-to-all-start.2 = ((bf16[8,256,8]{1,0,2:T(8,128)(2,1)}), bf16[8,256,8]{1,0,2:T(8,128)(2,1)S(1)}, u32[]{:S(2)}, u32[]{:S(2)}) async-start(bf16[8,256,8]{1,0,2:T(8,128)(2,1)} %broadcast_in_dim.24), calls=%async_computation.2 | async-start | bytes 65536 | tf_op jit(solution)/shard_map/all_to_all | solution.py:58
  25.9 50.4 %all-to-all-start = ((bf16[8,256,512]{1,0,2:T(8,128)(2,1)}), bf16[8,256,512]{1,0,2:T(8,128)(2,1)S(1)}, u32[]{:S(2)}, u32[]{:S(2)}) async-start(bf16[8,256,512]{1,0,2:T(8,128)(2,1)} %copy.25), calls=%async_computation | async-start | bytes 4194304 | tf_op jit(solution)/shard_map/all_to_all | solution.py:56
  76.3 52.0 %all-to-all-start.3 = ((bf16[8,256,512]{1,0,2:T(8,128)(2,1)}), bf16[8,256,512]{1,0,2:T(8,128)(2,1)}, u32[]{:S(2)}, u32[]{:S(2)}) async-start(bf16[8,256,512]{1,0,2:T(8,128)(2,1)} %copy.28), calls=%async_computation.3 | async-start | bytes 4194304 | tf_op jit(solution)/shard_map/all_to_all | solution.py:54
  128.3 52.2 %all-to-all-start.4 = ((bf16[8,256,512]{1,0,2:T(8,128)(2,1)}), bf16[8,256,512]{1,0,2:T(8,128)(2,1)}, u32[]{:S(2)}, u32[]{:S(2)}) async-start(bf16[8,256,512]{1,0,2:T(8,128)(2,1)} %copy.31), calls=%async_computation.4 | async-start | bytes 4194304 | tf_op jit(solution)/shard_map/all_to_all | solution.py:55
  141.3 44.2 %copy-start.1 = (bf16[8,2048,64]{1,2,0:T(8,128)(2,1)S(1)}, bf16[8,2048,64]{1,2,0:T(8,128)(2,1)}, u32[]{:S(2)}) copy-start(bf16[8,2048,64]{1,2,0:T(8,128)(2,1)} %custom-call) | copy-start | bytes 6291460
  191.2 3.9 copy-start
  210.0 3.9 copy-start
  228.9 3.9 copy-start
  247.7 3.9 copy-start
  266.6 3.9 copy-start
  285.4 3.9 copy-start
  304.2 3.9 copy-start
  323.1 3.9 copy-start
where the time goes:
time: 415 us; the launch traced here: 413 us
  waiting for transfers between devices  133 us (32%)
  matrix products  122 us (29%)
  local copies, waits for them, and re-layouts  54 us (13%)
  blocking collectives  51.8 us (12%)
  other arithmetic  29 us (7%)
  starting transfers between devices  23.1 us (6%)
    dot_general x32, matrix products, attend_dense(): jnp.einsum('qhd,khd->hqk', query_heads[offset:offset + query_span], key_h...  75.9 us
    all_to_all x1, blocking collectives, local(): lax.all_to_all(shortened(attended), 'seq', split_axis=1, concat_axis=2, t...  51.8 us
    dot_general x32, matrix products, attend_dense(): jnp.einsum('hqk,khd->qhd', weights, value_heads, preferred_element_type=j...  45.9 us
    all_to_all x1, waiting for transfers between devices, local(): lax.all_to_all(queries, 'seq', split_axis=2, concat_axis=1, tiled=True)  43.1 us
    all_to_all x1, waiting for transfers between devices, local(): lax.all_to_all(enc_values, 'seq', split_axis=2, concat_axis=1, tiled=True)  42.1 us
    all_to_all x1, waiting for transfers between devices, local(): lax.all_to_all(enc_keys, 'seq', split_axis=2, concat_axis=1, tiled=True)  39.2 us
    reduce_sum x8, other arithmetic, attend_dense(): row_total = jnp.sum(expos, axis=2, keepdims=True)  27.4 us
    unnamed x7, local copies, waits for them, and re-layouts  27.3 us
  transfers between devices with their start and end apart: 5, of which 5 were waited for; matrix products, arithmetic and copies ran while one was open for 6% of the time, Pallas kernels for 0%

commit v1 on v0

--- a/solution.py
+++ b/solution.py
@@ -5,6 +5,12 @@
 
 HEAD_DIM = 64
 masked_score = -1e30
+
+
+def stacked_exchange(array, axis, split, join):
+    pieces = jnp.split(array, lax.axis_size(axis), axis=split)
+    received = lax.all_to_all(jnp.stack(pieces), axis, 0, 0)
+    return jnp.concatenate(received, axis=join)
 
 
 def shortened(value):
@@ -68,9 +74,7 @@
         return attend_dense(members[0], members[1], members[2], members[3], members[4], head_count)
 
     attended = lax.map(one_row, (query_rows, key_rows, value_rows, dec_rows, enc_rows))
-    return lax.all_to_all(
-        shortened(attended), "seq", split_axis=1, concat_axis=2, tiled=True
-    ).astype(attended.dtype)
+    return stacked_exchange(shortened(attended), "seq", 1, 2).astype(attended.dtype)
 
 
 def solution(mesh):

time: 415 us -> 392 us (0.945)
  local copies, waits for them, and re-layouts: 54 us -> 31.9 us
    unnamed x7 -> x12, local copies, waits for them, and re-layouts: 27.3 us -> 13.8 us
    all_to_all x2 -> x1, local copies, waits for them, and re-layouts: 6.84 us -> 0.14 us  [stacked_exchange(): received = lax.all_to_all(jnp.stack(pieces), axis, 0, 0)]
    while x4 -> x3, local copies, waits for them, and re-layouts: 17.8 us -> 13.5 us  [local(): lax.map(one_row, (query_rows, key_rows, value_rows, dec_rows, enc_rows))]
where the time goes in v1:
time: 392 us; the launch traced here: 391 us
  waiting for transfers between devices  133 us (34%)
  matrix products  122 us (31%)
  blocking collectives  51.7 us (13%)
  local copies, waits for them, and re-layouts  31.9 us (8%)
  other arithmetic  29 us (7%)
  starting transfers between devices  23.1 us (6%)
    dot_general x32, matrix products, attend_dense(): jnp.einsum('qhd,khd->hqk', query_heads[offset:offset + query_span], key_h...  75.9 us
    all_to_all x1, blocking collectives, stacked_exchange(): received = lax.all_to_all(jnp.stack(pieces), axis, 0, 0)  51.7 us
    dot_general x32, matrix products, attend_dense(): jnp.einsum('hqk,khd->qhd', weights, value_heads, preferred_element_type=j...  45.9 us
    all_to_all x1, waiting for transfers between devices, local(): lax.all_to_all(queries, 'seq', split_axis=2, concat_axis=1, tiled=True)  43.1 us
    all_to_all x1, waiting for transfers between devices, local(): lax.all_to_all(enc_values, 'seq', split_axis=2, concat_axis=1, tiled=True)  42.1 us
    all_to_all x1, waiting for transfers between devices, local(): lax.all_to_all(enc_keys, 'seq', split_axis=2, concat_axis=1, tiled=True)  39.2 us
    reduce_sum x8, other arithmetic, attend_dense(): row_total = jnp.sum(expos, axis=2, keepdims=True)  27.4 us
    unnamed x12, local copies, waits for them, and re-layouts  13.8 us
  transfers between devices with their start and end apart: 5, of which 5 were waited for; matrix products, arithmetic and copies ran while one was open for 6% of the time, Pallas kernels for 0%

profile of v1, /device:TPU:0, one launch (start us, length us, event | category | flops | bytes accessed | tf_op | source)
XLA Modules:
  0.0 390.8 jit_solution(16948654742915008345)
XLA Ops:
  1.3 7.3 %all-to-all-start.1 = ((bf16[8,256,8]{1,0,2:T(8,128)(2,1)}), bf16[8,256,8]{1,0,2:T(8,128)(2,1)S(1)}, u32[]{:S(2)}, u32[]{:S(2)}) async-start(bf16[8,256,8]{1,0,2:T(8,128)(2,1)} %broadcast_in_dim.23), calls=%async_computation.1 | async-start | bytes 65536 | tf_op jit(solution)/shard_map/all_to_all | solution.py:63
  9.3 6.0 %all-to-all-done.1 = bf16[8,256,8]{1,0,2:T(8,128)(2,1)S(1)} async-done(((bf16[8,256,8]{1,0,2:T(8,128)(2,1)}), bf16[8,256,8]{1,0,2:T(8,128)(2,1)S(1)}, u32[]{:S(2)}, u32[]{:S(2)}) %all-to-all-start.1) | async-done | bytes 32800 | tf_op jit(solution)/shard_map/all_to_all | solution.py:63
  19.2 4.5 %copy.24 = bf16[8,256,512]{1,0,2:T(8,128)(2,1)} copy(bf16[8,256,512]{2,1,0:T(8,128)(2,1)} %param.9) | data formatting | bytes 4194304 | tf_op args[2]
  25.9 3.8 all-to-all-start
  29.7 4.5 %copy.27 = bf16[8,256,512]{1,0,2:T(8,128)(2,1)} copy(bf16[8,256,512]{2,1,0:T(8,128)(2,1)} %param.7) | data formatting | bytes 4194304 | tf_op args[0]
  34.2 42.1 %all-to-all-done = bf16[8,256,512]{1,0,2:T(8,128)(2,1)S(1)} async-done(((bf16[8,256,512]{1,0,2:T(8,128)(2,1)}), bf16[8,256,512]{1,0,2:T(8,128)(2,1)S(1)}, u32[]{:S(2)}, u32[]{:S(2)}) %all-to-all-start) | async-done | bytes 2097184 | tf_op jit(solution)/shard_map/all_to_all | solution.py:62
  76.3 4.4 %all-to-all-start.3 = ((bf16[8,256,512]{1,0,2:T(8,128)(2,1)}), bf16[8,256,512]{1,0,2:T(8,128)(2,1)}, u32[]{:S(2)}, u32[]{:S(2)}) async-start(bf16[8,256,512]{1,0,2:T(8,128)(2,1)} %copy.27), calls=%async_computation.3 | async-start | bytes 4194304 | tf_op jit(solution)/shard_map/all_to_all | solution.py:60
  80.7 4.5 %copy.30 = bf16[8,256,512]{1,0,2:T(8,128)(2,1)} copy(bf16[8,256,512]{2,1,0:T(8,128)(2,1)} %param.8) | data formatting | bytes 4194304 | tf_op args[1]
  85.2 43.1 %all-to-all-done.3 = bf16[8,256,512]{1,0,2:T(8,128)(2,1)} async-done(((bf16[8,256,512]{1,0,2:T(8,128)(2,1)}), bf16[8,256,512]{1,0,2:T(8,128)(2,1)}, u32[]{:S(2)}, u32[]{:S(2)}) %all-to-all-start.3) | async-done | bytes 2097184 | tf_op jit(solution)/shard_map/all_to_all | solution.py:60
  128.3 4.4 %all-to-all-start.4 = ((bf16[8,256,512]{1,0,2:T(8,128)(2,1)}), bf16[8,256,512]{1,0,2:T(8,128)(2,1)}, u32[]{:S(2)}, u32[]{:S(2)}) async-start(bf16[8,256,512]{1,0,2:T(8,128)(2,1)} %copy.30), calls=%async_computation.4 | async-start | bytes 4194304 | tf_op jit(solution)/shard_map/all_to_all | solution.py:61
  132.7 3.5 copy.39
  136.3 5.0 %copy.41 = bf16[8,8,256,64]{3,2,1,0:T(8,128)(2,1)} copy(bf16[8,8,256,64]{2,0,3,1:T(8,128)(2,1)} %bitcast.36) | data formatting | bytes 4194304 | tf_op jit(solution)/shard_map/while | solution.py:76
  141.3 39.2 %all-to-all-done.4 = bf16[8,256,512]{1,0,2:T(8,128)(2,1)} async-done(((bf16[8,256,512]{1,0,2:T(8,128)(2,1)}), bf16[8,256,512]{1,0,2:T(8,128)(2,1)}, u32[]{:S(2)}, u32[]{:S(2)}) %all-to-all-start.4) | async-done | bytes 2097184 | tf_op jit(solution)/shard_map/all_to_all | solution.py:61
  180.5 5.0 %copy.43 = bf16[8,8,256,64]{3,2,1,0:T(8,128)(2,1)} copy(bf16[8,8,256,64]{2,0,3,1:T(8,128)(2,1)} %bitcast.40) | data formatting | bytes 4194304 | tf_op jit(solution)/shard_map/while | solution.py:76
  185.5 150.7 %while.10 = (s32[]{:T(128)}, bf16[8,2048,64]{1,2,0:T(8,128)(2,1)S(1)}, bf16[8,2048,64]{2,1,0:T(8,128)(2,1)}, s32[8,2048]{1,0:T(8,128)S(1)}, s32[8,2048]{1,0:T(8,...) while((s32[]{:T(128)}, ...), condition=%wide.region_9.10_spmd, body=%wide.region_0.9_spmd.sunk | while | flops 1133637632 | bytes 72773864 | solution.py:76
  191.2 3.9 fusion.85
  210.1 3.9 fusion.85
  228.9 3.9 fusion.85
  247.7 3.9 fusion.85
  266.6 3.9 fusion.85
  285.4 3.9 fusion.85
  304.2 3.9 fusion.85
  323.1 3.9 fusion.85
  336.5 51.7 %all_to_all.77 = bf16[8,8,256,64]{2,3,1,0:T(8,128)(2,1)S(1)} all-to-all(bf16[8,8,256,64]{2,3,1,0:T(8,128)(2,1)S(1)} %bitcast_dynamic-update-slice_fusion), channel_id=1, replica_groups=mesh['dp'=4,'seq'=8] {'seq'}, dimensions={0} | all-to-all | bytes 4194304 | tf_op jit(solution)/shard_map/all_to_all | solution.py:12
  (125 shorter events, 130.1 us)
Async XLA Ops:
  1.3 14.0 %all-to-all-start.1 = ((bf16[8,256,8]{1,0,2:T(8,128)(2,1)}), bf16[8,256,8]{1,0,2:T(8,128)(2,1)S(1)}, u32[]{:S(2)}, u32[]{:S(2)}) async-start(bf16[8,256,8]{1,0,2:T(8,128)(2,1)} %broadcast_in_dim.23), calls=%async_computation.1 | async-start | bytes 65536 | tf_op jit(solution)/shard_map/all_to_all | solution.py:63
  15.9 10.0 %all-to-all-start.2 = ((bf16[8,256,8]{1,0,2:T(8,128)(2,1)}), bf16[8,256,8]{1,0,2:T(8,128)(2,1)S(1)}, u32[]{:S(2)}, u32[]{:S(2)}) async-start(bf16[8,256,8]{1,0,2:T(8,128)(2,1)} %broadcast_in_dim.24), calls=%async_computation.2 | async-start | bytes 65536 | tf_op jit(solution)/shard_map/all_to_all | solution.py:64
  25.9 50.4 %all-to-all-start = ((bf16[8,256,512]{1,0,2:T(8,128)(2,1)}), bf16[8,256,512]{1,0,2:T(8,128)(2,1)S(1)}, u32[]{:S(2)}, u32[]{:S(2)}) async-start(bf16[8,256,512]{1,0,2:T(8,128)(2,1)} %copy.24), calls=%async_computation | async-start | bytes 4194304 | tf_op jit(solution)/shard_map/all_to_all | solution.py:62
  76.3 52.0 %all-to-all-start.3 = ((bf16[8,256,512]{1,0,2:T(8,128)(2,1)}), bf16[8,256,512]{1,0,2:T(8,128)(2,1)}, u32[]{:S(2)}, u32[]{:S(2)}) async-start(bf16[8,256,512]{1,0,2:T(8,128)(2,1)} %copy.27), calls=%async_computation.3 | async-start | bytes 4194304 | tf_op jit(solution)/shard_map/all_to_all | solution.py:60
  128.3 52.2 %all-to-all-start.4 = ((bf16[8,256,512]{1,0,2:T(8,128)(2,1)}), bf16[8,256,512]{1,0,2:T(8,128)(2,1)}, u32[]{:S(2)}, u32[]{:S(2)}) async-start(bf16[8,256,512]{1,0,2:T(8,128)(2,1)} %copy.30), calls=%async_computation.4 | async-start | bytes 4194304 | tf_op jit(solution)/shard_map/all_to_all | solution.py:61
  141.3 44.2 %copy-start.1 = (bf16[8,2048,64]{1,2,0:T(8,128)(2,1)S(1)}, bf16[8,2048,64]{1,2,0:T(8,128)(2,1)}, u32[]{:S(2)}) copy-start(bf16[8,2048,64]{1,2,0:T(8,128)(2,1)} %custom-call.1) | copy-start | bytes 6291460
  191.2 3.9 copy-start
  210.0 3.9 copy-start
  228.9 3.9 copy-start
  247.7 3.9 copy-start
  266.6 3.9 copy-start
  285.4 3.9 copy-start
  304.2 3.9 copy-start
  323.1 3.9 copy-start
